TPU v7x, 32 devices: a whole 2x2x4 slice. The times are simulated.
32 devices in a mesh: chan: 4 (over z), pulse: 4 (over x, core), range: 2 (over y).
Axes of the slice: x: 2, y: 2, z: 4, core: 2. Of those that a mesh axis runs over, the one named last changes fastest.
Arguments:
- signal: bfloat16 [2, 64, 32, 8192], P(None, 'chan', 'pulse', 'range'), may hold values from -6 to 6
- steering: bfloat16 [2, 32, 64], replicated, may hold values from -0.5 to 0.5
- spectrum: float32 [2, 8192], replicated, may hold values from -6 to 6
Outputs:
- detection: float32 [32, 32, 8192], P('chan', 'pulse', 'range')
All inputs are finite; a program needn't handle non-finite values.
Results may differ from a plain program's by a relative error of at most 0.0087.
Values may be sent and summed in bfloat16 or wider, within the bound.
A program may use at most 64 MiB of HBM per device.

v0:
```python
import math
import jax
import jax.numpy as jnp
from jax import lax
from jax.sharding import PartitionSpec as P

GUARD = 4
TRAIN = 16
PRECISE = lax.Precision.HIGHEST
NOISE_FLOOR = 0.25


def padded_2(x, sides, width):
    for axis, dim in sides:
        peers, length = (lax.axis_size(axis), x.shape[dim])
        up = [(i, (i + 1) % peers) for i in range(peers - 1)]
        down = [(j, i) for i, j in up]
        last = lax.slice_in_dim(x, length - width, length, axis=dim)
        initial = lax.slice_in_dim(x, 0, width, axis=dim)
        before = lax.ppermute(last, axis, up)
        after = lax.ppermute(initial, axis, down)
        x = jnp.concatenate([before, x, after], axis=dim)
    return x


def doppler_tables(pulse_count):
    row_ids = lax.broadcasted_iota(jnp.int32, (pulse_count, pulse_count), 0)
    col_ids = lax.broadcasted_iota(jnp.int32, (pulse_count, pulse_count), 1)
    phase_angle = (row_ids * col_ids % pulse_count).astype(jnp.float32) * (
        2.0 * math.pi / pulse_count
    )
    norm_scale = 1.0 / math.sqrt(pulse_count)
    table_real = (jnp.cos(phase_angle) * norm_scale).astype(jnp.bfloat16)
    table_imag = (-jnp.sin(phase_angle) * norm_scale).astype(jnp.bfloat16)
    return (table_real, table_imag)


def phase_table(row_count, col_count, period_len, direction):
    row_ids = lax.broadcasted_iota(jnp.int32, (row_count, col_count), 0)
    col_ids = lax.broadcasted_iota(jnp.int32, (row_count, col_count), 1)
    phase_angle = (row_ids * col_ids % period_len).astype(jnp.float32) * (
        2.0 * math.pi / period_len
    )
    return (jnp.cos(phase_angle), direction * jnp.sin(phase_angle))


def rotate_by(field_pair, table_pair):
    return (
        field_pair[0] * table_pair[0] - field_pair[1] * table_pair[1],
        field_pair[0] * table_pair[1] + field_pair[1] * table_pair[0],
    )


def mix_blocks(table_pair, field_pair):

    def contract(table_part, field_part):
        return jnp.einsum("km,bpmn->bpkn", table_part, field_part, precision=PRECISE)

    return (
        contract(table_pair[0], field_pair[0]) - contract(table_pair[1], field_pair[1]),
        contract(table_pair[0], field_pair[1]) + contract(table_pair[1], field_pair[0]),
    )


def mix_lanes(field_pair, table_pair):

    def contract(field_part, table_part):
        return jnp.einsum("bpkm,mn->bpkn", field_part, table_part, precision=PRECISE)

    return (
        contract(field_pair[0], table_pair[0]) - contract(field_pair[1], table_pair[1]),
        contract(field_pair[0], table_pair[1]) + contract(field_pair[1], table_pair[0]),
    )


def local_transform(field_pair, direction):
    size_all = field_pair[0].shape[-1]
    blocks = size_all // 128
    leading = field_pair[0].shape[:-1]
    shaped = tuple((member.reshape(leading + (blocks, 128)) for member in field_pair))
    outer_table = phase_table(blocks, blocks, blocks, direction)
    twiddle = phase_table(blocks, 128, size_all, direction)
    inner_table = phase_table(128, 128, 128, direction)
    if direction < 0:
        shaped = mix_blocks(outer_table, shaped)
        shaped = rotate_by(shaped, twiddle)
        shaped = mix_lanes(shaped, inner_table)
    else:
        shaped = mix_lanes(shaped, inner_table)
        shaped = rotate_by(shaped, twiddle)
        shaped = mix_blocks(outer_table, shaped)
    return tuple((member.reshape(leading + (size_all,)) for member in shaped))


def stack_weights(w_real, w_imag):
    return jnp.concatenate(
        [jnp.concatenate([w_real, -w_imag], 1), jnp.concatenate([w_imag, w_real], 1)], 0
    )


def shards(signal, steering, spectrum):
    beam_count = steering.shape[1]
    chan_count = steering.shape[2]
    pulse_local = signal.shape[2]
    gate_count = signal.shape[3]
    stacked = stack_weights(steering[0], steering[1])
    samples = lax.all_to_all(signal, "chan", split_axis=2, concat_axis=1, tiled=True)
    pulses_here = samples.shape[2]
    gates_here = samples.shape[3]
    flat_samples = samples.reshape(2 * chan_count, pulses_here * gates_here)
    formed = jnp.dot(stacked, flat_samples, preferred_element_type=jnp.float32)
    formed = formed.astype(jnp.bfloat16).reshape(2, beam_count, pulses_here, gates_here)
    beam_data = lax.all_to_all(formed, "chan", split_axis=1, concat_axis=2, tiled=True)
    beam_local = beam_data.shape[1]
    range_count = lax.axis_size("range")
    range_index = lax.axis_index("range")
    full_length = gate_count * range_count
    inverse_scale = 1.0 / full_length
    shard_piece = lax.all_gather(beam_data, "range", axis=3, tiled=True)
    shard_count = shard_piece.shape[3] // gate_count
    members = shard_piece.astype(jnp.float32).reshape(
        2, beam_local, pulse_local, shard_count, gate_count
    )
    source = jnp.arange(shard_count, dtype=jnp.int32)
    phase_angle = (source * range_index % range_count).astype(jnp.float32) * (
        2.0 * math.pi / range_count
    )
    cos_part = jnp.cos(phase_angle)[:, None]
    sin_part = -jnp.sin(phase_angle)[:, None]
    sum_real = jnp.sum(members[0] * cos_part - members[1] * sin_part, axis=2)
    sum_imag = jnp.sum(members[0] * sin_part + members[1] * cos_part, axis=2)
    folded = (sum_real, sum_imag)
    gate_ids = lax.broadcasted_iota(jnp.int32, (gate_count,), 0)
    global_angle = (gate_ids * range_index % full_length).astype(jnp.float32) * (
        2.0 * math.pi / full_length
    )
    folded = rotate_by(folded, (jnp.cos(global_angle), -jnp.sin(global_angle)))
    spectrum_local = local_transform(folded, -1.0)
    response = spectrum.reshape(2, gate_count, range_count)
    response = lax.dynamic_index_in_dim(response, range_index, axis=2, keepdims=False)
    response = jnp.transpose(response.reshape(2, 128, gate_count // 128), (0, 2, 1)).reshape(
        2, gate_count
    )
    filtered = rotate_by(spectrum_local, (response[0], response[1]))
    restored = local_transform(filtered, 1.0)
    restored = rotate_by(restored, (jnp.cos(global_angle), jnp.sin(global_angle)))
    shard_piece = (
        lax.all_gather(restored[0], "range", axis=2, tiled=True),
        lax.all_gather(restored[1], "range", axis=2, tiled=True),
    )
    shard_count = shard_piece[0].shape[2] // gate_count
    rows_real = shard_piece[0].reshape(beam_local, pulse_local, shard_count, gate_count)
    rows_imag = shard_piece[1].reshape(beam_local, pulse_local, shard_count, gate_count)
    source = jnp.arange(shard_count, dtype=jnp.int32)
    phase_angle = (source * range_index % range_count).astype(jnp.float32) * (
        2.0 * math.pi / range_count
    )
    cos_part = jnp.cos(phase_angle)[:, None]
    sin_part = jnp.sin(phase_angle)[:, None]
    sum_real = jnp.sum(rows_real * cos_part - rows_imag * sin_part, axis=2)
    sum_imag = jnp.sum(rows_real * sin_part + rows_imag * cos_part, axis=2)
    compressed = jnp.stack([sum_real * inverse_scale, sum_imag * inverse_scale]).astype(
        jnp.bfloat16
    )
    pulse_total = pulse_local * lax.axis_size("pulse")
    dop_real, dop_imag = doppler_tables(pulse_total)
    columns = lax.all_to_all(compressed, "pulse", split_axis=3, concat_axis=2, tiled=True)

    def product(table_part, values):
        return jnp.einsum("fp,bpr->bfr", table_part, values, preferred_element_type=jnp.float32)

    mixed_real = product(dop_real, columns[0]) - product(dop_imag, columns[1])
    mixed_imag = product(dop_real, columns[1]) + product(dop_imag, columns[0])
    power_part = lax.all_to_all(
        mixed_real * mixed_real + mixed_imag * mixed_imag,
        "pulse",
        split_axis=1,
        concat_axis=2,
        tiled=True,
    )
    halo_width = GUARD + TRAIN
    padded = padded_2(power_part, (("range", 2),), halo_width)
    window_sum = jnp.zeros_like(power_part)
    for offset in range(1, TRAIN + 1):
        left_start = halo_width - GUARD - offset
        right_start = halo_width + GUARD + offset
        window_sum = (
            window_sum
            + padded[:, :, left_start : left_start + gate_count]
            + padded[:, :, right_start : right_start + gate_count]
        )
    noise_level = window_sum / (2.0 * TRAIN)
    return power_part / (noise_level + NOISE_FLOOR)


def solution(mesh):
    in_specs = (P(None, "chan", "pulse", "range"), P(), P())
    out_specs = P("chan", "pulse", "range")
    return jax.shard_map(shards, mesh=mesh, in_specs=in_specs, out_specs=out_specs, check_vma=False)
```

profile of v0, /device:TPU:0, one launch (start us, length us, event | category | flops | bytes accessed | tf_op | source)
XLA Modules:
  0.0 388.4 jit_solution(4963313028370823325)
XLA Ops:
  6.5 4.1 %copy.81 = bf16[2,16,8,4096]{3,1,0,2:T(8,128)(2,1)} copy(bf16[2,16,8,4096]{3,2,1,0:T(8,128)(2,1)} %param.3) | data formatting | bytes 4194304 | tf_op args[0]
  10.6 6.5 %all-to-all-start = ((bf16[2,16,8,4096]{3,1,0,2:T(8,128)(2,1)}), bf16[2,16,8,4096]{3,1,0,2:T(8,128)(2,1)S(1)}, u32[]{:S(2)}, u32[]{:S(2)}) async-start(bf16[2,16,8,4096]{3,1,0,2:T(8,128)(2,1)} %copy.81), calls=%async_computation | async-start | bytes 4194304 | tf_op jit(solution)/shard_map/all_to_all | solution.py:107
  17.1 48.2 %all-to-all-done = bf16[2,16,8,4096]{3,1,0,2:T(8,128)(2,1)S(1)} async-done(((bf16[2,16,8,4096]{3,1,0,2:T(8,128)(2,1)}), bf16[2,16,8,4096]{3,1,0,2:T(8,128)(2,1)S(1)}, u32[]{:S(2)}, u32[]{:S(2)}) %all-to-all-start) | async-done | bytes 2097184 | tf_op jit(solution)/shard_map/all_to_all | solution.py:107
  65.3 2.2 copy.82
  71.0 27.7 %all_to_all.66 = bf16[2,32,2,4096]{3,2,0,1:T(2,128)(2,1)S(1)} all-to-all(bf16[2,32,2,4096]{3,2,0,1:T(2,128)(2,1)S(1)} %copy.83), channel_id=1, replica_groups=mesh['chan'=4,'pulse'=4,'range'=2] {'chan'}, dimensions={1} | all-to-all | bytes 2097152 | tf_op jit(solution)/shard_map/all_to_all | solution.py:113
  100.6 6.4 %reshape.188 = f32[2,4096,2]{2,1,0:T(8,128)} reshape(f32[2,8192]{1,0:T(2,128)S(1)} %copy-done.1) | data formatting | bytes 131072 | tf_op jit(solution)/shard_map/reshape | solution.py:139
  107.0 4.7 %dynamic-slice_reduce_fusion = f32[2,4096]{1,0:T(2,128)S(1)} fusion(f32[2,4096,2]{2,1,0:T(8,128)} %reshape.188, s32[]{:T(128)S(6)} %select_n.134), kind=kLoop, calls=%fused_computation.31 | loop fusion | bytes 65540 | tf_op jit(solution)/shard_map/jit(dynamic_index_in_dim)/dynamic_slice | solution.py:140
  112.5 20.2 %all-gather.4.cloned.1.call-done = bf16[2,8,8,8192]{3,1,2,0:T(8,128)(2,1)} async-done(((bf16[2,8,8,4096]{3,1,2,0:T(8,128)(2,1)}), bf16[2,8,8,8192]{3,1,2,0:T(8,128)(2,1)}) %all-gather.4.cloned.1.call-update) | async-done | bytes 2097168 | tf_op jit(solution)/shard_map/all_gather | solution.py:119
  132.7 3.9 %fusion.271 = (f32[1,8,8,8192]{3,1,2,0:T(8,128)}, f32[1,8,8,8192]{3,1,2,0:T(8,128)}) fusion(bf16[2,8,8,8192]{3,1,2,0:T(8,128)(2,1)} %all-gather.4.cloned.1.call-done), kind=kLoop, calls=%fused_computation.365 | loop fusion | bytes 8388608 | tf_op jit(solution)/shard_map/slice | solution.py:130
  136.6 3.0 reshape.202
  139.7 4.4 %reshape.203 = f32[8,8,2,4096]{3,2,0,1:T(2,128)} reshape(f32[1,8,8,8192]{3,1,2,0:T(8,128)} %get-tuple-element.12) | data formatting | bytes 4194304 | tf_op jit(solution)/shard_map/squeeze | solution.py:130
  144.1 5.8 %subtract_reduce_fusion.1 = (f32[8,8,4096]{2,1,0:T(8,128)S(1)}, f32[8,8,4096]{2,1,0:T(8,128)S(1)}) fusion(f32[8,8,2,4096]{3,2,0,1:T(2,128)} %reshape.203, f32[8,8,2,4096]{3,2,0,1:T(2,128)S(1)} %reshape.202, f32[2]{0:T(128)S(1)} %get-tuple-element.24, f32[2]{0:T(128)S(1)} %get-tuple-element.23), kind=kLoop, calls=%fused_computation.35 | loop fusion | flops 3670016 | bytes 6291472 | tf_op jit(solution)/shard_map/reduce_sum | solution.py:130
  152.6 1.5 fusion.84
  154.1 1.5 fusion.2
  155.6 1.5 fusion.3
  169.8 2.2 fusion
  172.0 2.4 reshape.191
  174.3 2.2 fusion.1
  176.5 1.5 reshape.190
  178.1 1.6 multiply_subtract_fusion
  180.4 32.5 %all-gather.6.cloned.1.call-done = f32[8,8,8192]{2,1,0:T(8,128)} async-done(((f32[8,8,4096]{2,1,0:T(8,128)}), f32[8,8,8192]{2,1,0:T(8,128)}) %all-gather.6.cloned.1.call-update) | async-done | bytes 2097168 | tf_op jit(solution)/shard_map/all_gather | solution.py:148
  212.9 34.7 %all-gather.8.cloned.1.call-done = f32[8,8,8192]{2,1,0:T(8,128)} async-done(((f32[8,8,4096]{2,1,0:T(8,128)}), f32[8,8,8192]{2,1,0:T(8,128)}) %all-gather.8.cloned.1.call-update) | async-done | bytes 2097168 | tf_op jit(solution)/shard_map/all_gather | solution.py:149
  247.6 3.2 subtract_reduce_fusion
  252.1 14.0 %copy.106 = bf16[2,8,8,4096]{2,1,0,3:T(8,128)(2,1)} copy(bf16[2,8,8,4096]{3,1,2,0:T(8,128)(2,1)S(1)} %pad_maximum_fusion.2) | data formatting | bytes 2097152 | tf_op jit(solution)/shard_map/stack | solution.py:162
  266.1 20.5 %reshape.205 = bf16[4,2,65536]{2,1,0:T(2,128)(2,1)S(1)} reshape(bf16[4096,2,8,8]{3,2,1,0:T(8,128)(2,1)} %bitcast.133) | data formatting | bytes 2097152
  286.6 17.2 %all_to_all.67 = bf16[4,2,65536]{2,1,0:T(2,128)(2,1)S(1)} all-to-all(bf16[4,2,65536]{2,1,0:T(2,128)(2,1)S(1)} %reshape.205), channel_id=1, replica_groups=mesh['chan'=4,'pulse'=4,'range'=2] {'pulse'}, dimensions={0} | all-to-all | bytes 2097152 | tf_op jit(solution)/shard_map/all_to_all | solution.py:167
  303.8 21.7 %reshape.206 = bf16[4096,2,8,8]{3,2,1,0:T(8,128)(2,1)} reshape(bf16[4,2,65536]{2,1,0:T(2,128)(2,1)S(1)} %all_to_all.67) | data formatting | bytes 2097152
  325.5 16.0 %copy.107 = bf16[2,8,8,4,1024]{4,2,3,1,0:T(8,128)(2,1)S(1)} copy(bf16[2,8,8,4,1024]{2,1,0,4,3:T(8,128)(2,1)} %bitcast.134) | data formatting | bytes 2097152 | tf_op jit(solution)/shard_map/all_to_all | solution.py:167
  343.6 16.9 %all_to_all.68 = f32[8,32,1024]{2,0,1:T(8,128)S(1)} all-to-all(f32[8,32,1024]{2,0,1:T(8,128)S(1)} %copy.108), channel_id=1, replica_groups=mesh['chan'=4,'pulse'=4,'range'=2] {'pulse'}, dimensions={1} | all-to-all | bytes 2097152 | tf_op jit(solution)/shard_map/all_to_all | solution.py:174
  361.2 2.4 collective-permute-start
  365.2 4.2 %collective-permute-done.1 = f32[8,8,20]{2,1,0:T(8,128)S(1)} collective-permute-done((f32[8,8,20]{2,1,0:T(8,128)S(1)}, f32[8,8,20]{2,1,0:T(8,128)S(1)}, u32[]{:S(2)}, u32[]{:S(2)}) %collective-permute-start.1) | collective-permute-done | bytes 5152 | tf_op jit(solution)/shard_map/ppermute | solution.py:21
  369.4 12.0 %fusion.14 = f32[8,8,4096]{2,1,0:T(8,128)} fusion(f32[8,8,4096]{2,1,0:T(8,128)S(1)} %bitcast.151, f32[8,8,20]{2,1,0:T(8,128)S(1)} %collective-permute-done.1, f32[8,8,20]{2,1,0:T(8,128)S(1)} %collective-permute-done), kind=kLoop, calls=%fused_computation.60 | loop fusion | flops 17301504 | bytes 2107392 | tf_op jit(solution)/shard_map/div | solution.py:193
  (55 shorter events, 27.8 us)
Async XLA Ops:
  10.6 6.5 %copy-start.2 = (bf16[2,32,64]{2,1,0:T(8,128)(2,1)S(1)}, bf16[2,32,64]{2,1,0:T(8,128)(2,1)}, u32[]{:S(2)}) copy-start(bf16[2,32,64]{2,1,0:T(8,128)(2,1)} %param.4) | copy-start | bytes 24580
  10.6 54.7 %all-to-all-start = ((bf16[2,16,8,4096]{3,1,0,2:T(8,128)(2,1)}), bf16[2,16,8,4096]{3,1,0,2:T(8,128)(2,1)S(1)}, u32[]{:S(2)}, u32[]{:S(2)}) async-start(bf16[2,16,8,4096]{3,1,0,2:T(8,128)(2,1)} %copy.81), calls=%async_computation | async-start | bytes 4194304 | tf_op jit(solution)/shard_map/all_to_all | solution.py:107
  17.1 115.6 %all-gather.4.cloned.1.call-start = ((), (), s32[]{:S(2)}) async-start(), calls=%async_computation.4 | async-start | bytes 3145728 | tf_op jit(solution)/shard_map/all_gather | solution.py:119
  99.3 1.3 copy-start.1
  100.4 112.5 %all-gather.6.cloned.1.call-start = ((), (), s32[]{:S(2)}) async-start(), calls=%async_computation.5 | async-start | bytes 3145728 | tf_op jit(solution)/shard_map/all_gather | solution.py:148
  176.5 1.5 copy-start
  179.7 67.9 %all-gather.8.cloned.1.call-start = ((), (), s32[]{:S(2)}) async-start(), calls=%async_computation.6 | async-start | bytes 3145728 | tf_op jit(solution)/shard_map/all_gather | solution.py:149
  361.2 4.0 %collective-permute-start = (f32[8,8,20]{2,1,0:T(8,128)S(1)}, f32[8,8,20]{2,1,0:T(8,128)S(1)}, u32[]{:S(2)}, u32[]{:S(2)}) collective-permute-start(f32[8,8,20]{2,1,0:T(8,128)S(1)} %get-tuple-element.13), channel_id=1, source_target_pairs={{0,1},{2,3},{4,5},{6,7},{8,9},{10,11},{12,13},{14,15},{16,17},{18,... | collective-permute-start | bytes 15368 | tf_op jit(solution)/shard_map/ppermute | solution.py:20
  363.6 5.8 %collective-permute-start.1 = (f32[8,8,20]{2,1,0:T(8,128)S(1)}, f32[8,8,20]{2,1,0:T(8,128)S(1)}, u32[]{:S(2)}, u32[]{:S(2)}) collective-permute-start(f32[8,8,20]{2,1,0:T(8,128)S(1)} %get-tuple-element.14), channel_id=1, source_target_pairs={{1,0},{3,2},{5,4},{7,6},{9,8},{11,10},{13,12},{15,14},{17,16},{19,... | collective-permute-start | bytes 15368 | tf_op jit(solution)/shard_map/ppermute | solution.py:21
Sparse Core Ops, SparseCore 0:
  100.5 32.1 all-gather.3
  179.8 33.0 all-gather.5
  214.5 33.0 all-gather.7
where the time goes:
time: 395 us; the launch traced here: 388 us
  waiting for transfers between devices  141 us (36%)
  local copies, waits for them, and re-layouts  112 us (28%)
  blocking collectives  61.8 us (16%)
  matrix products  24.9 us (6%)
  other arithmetic  24.3 us (6%)
  between operations  13.9 us (4%)
  starting transfers between devices  10.5 us (3%)
    unnamed x12, local copies, waits for them, and re-layouts  48.9 us
    all_to_all x1, waiting for transfers between devices, shards(): lax.all_to_all(signal, 'chan', split_axis=2, concat_axis=1, tiled=True)  48.2 us
    all_gather x1, waiting for transfers between devices, shards(): lax.all_gather(restored[1], 'range', axis=2, tiled=True)  34.7 us
    all_gather x1, waiting for transfers between devices, shards(): lax.all_gather(restored[0], 'range', axis=2, tiled=True)  32.5 us
    all_to_all x1, blocking collectives, shards(): lax.all_to_all(formed, 'chan', split_axis=1, concat_axis=2, tiled=True)  27.7 us
    all_gather x1, waiting for transfers between devices, shards(): shard_piece = lax.all_gather(beam_data, 'range', axis=3, tiled=True)  20.2 us
    all_to_all x1, blocking collectives, shards(): lax.all_to_all(compressed, 'pulse', split_axis=3, concat_axis=2, tiled=True)  17.2 us
    all_to_all x1, blocking collectives, shards(): lax.all_to_all(mixed_real * mixed_real + mixed_imag * mixed_imag, 'pulse'...  16.9 us
  transfers between devices with their start and end apart: 6, of which 6 were waited for; matrix products, arithmetic and copies ran while one was open for 3% of the time, Pallas kernels for 0%

commit v1 on v0

--- a/solution.py
+++ b/solution.py
@@ -8,6 +8,17 @@
 TRAIN = 16
 PRECISE = lax.Precision.HIGHEST
 NOISE_FLOOR = 0.25
+
+
+def cut_along(value, dim, peers):
+    before, after = (value.shape[:dim], value.shape[dim + 1 :])
+    return jnp.moveaxis(value.reshape(*before, peers, -1, *after), dim, 0)
+
+
+def in_order(parts, dim):
+    dims = list(parts.shape[1:])
+    dims[dim] *= parts.shape[0]
+    return jnp.moveaxis(parts, 0, dim).reshape(dims)
 
 
 def padded_2(x, sides, width):
@@ -110,7 +121,17 @@
     flat_samples = samples.reshape(2 * chan_count, pulses_here * gates_here)
     formed = jnp.dot(stacked, flat_samples, preferred_element_type=jnp.float32)
     formed = formed.astype(jnp.bfloat16).reshape(2, beam_count, pulses_here, gates_here)
-    beam_data = lax.all_to_all(formed, "chan", split_axis=1, concat_axis=2, tiled=True)
+    size, mine = (lax.axis_size("chan"), lax.axis_index("chan"))
+    tiles = cut_along(formed, 1, size)
+    out = tiles
+    for lap in range(1, size):
+        target, source_2 = ((mine + lap) % size, (mine - lap) % size)
+        sent = lax.dynamic_index_in_dim(tiles, target, 0)
+        partner_block = lax.ppermute(
+            sent, "chan", [(i_2, (i_2 + lap) % size) for i_2 in range(size)]
+        )
+        out = lax.dynamic_update_slice_in_dim(out, partner_block, source_2, axis=0)
+    beam_data = in_order(out, 2)
     beam_local = beam_data.shape[1]
     range_count = lax.axis_size("range")
     range_index = lax.axis_index("range")

time: 395 us -> 396 us (level)
  blocking collectives: 61.8 us -> 34.1 us
  waiting for transfers between devices: 141 us -> 157 us
  other arithmetic: 24.3 us -> 30 us
  local copies, waits for them, and re-layouts: 112 us -> 116 us
    all_to_all x1 -> x0, blocking collectives: 27.7 us -> none  [shards(): lax.all_to_all(formed, 'chan', split_axis=1, concat_axis=2, tiled=True)]
    ppermute x0 -> x3, waiting for transfers between devices: none -> 19.9 us  [shards(): lax.ppermute(sent, 'chan', [(i_2, (i_2 + lap) % size) for i_2 in range(si...]
    reshape x2 -> x3, local copies, waits for them, and re-layouts: 1.7 us -> 8.79 us  [the longest x1 4.03 us: shards(): shard_piece[1].reshape(beam_local, pulse_local, shard_count, gate_count)]
    reduce_sum x1, other arithmetic: 3.16 us -> 7.61 us  [shards(): sum_real = jnp.sum(rows_real * cos_part - rows_imag * sin_part, axis=2)]
    unnamed x12 -> x10, local copies, waits for them, and re-layouts: 48.9 us -> 47.7 us
  transfers between devices with their start and end apart: 6 -> 9, of which waited for: 6 -> 8; matrix products, arithmetic and copies ran while one was open for 3% -> 4% of each run, Pallas kernels for 0% -> 0%
where the time goes in v1:
time: 396 us; the launch traced here: 390 us
  waiting for transfers between devices  157 us (40%)
  local copies, waits for them, and re-layouts  116 us (29%)
  blocking collectives  34.1 us (9%)
  other arithmetic  30 us (8%)
  matrix products  24.3 us (6%)
  starting transfers between devices  14.3 us (4%)
  between operations  14 us (4%)
    all_to_all x1, waiting for transfers between devices, shards(): lax.all_to_all(signal, 'chan', split_axis=2, concat_axis=1, tiled=True)  48.2 us
    unnamed x10, local copies, waits for them, and re-layouts  47.7 us
    all_gather x1, waiting for transfers between devices, shards(): lax.all_gather(restored[0], 'range', axis=2, tiled=True)  32.5 us
    all_gather x1, waiting for transfers between devices, shards(): lax.all_gather(restored[1], 'range', axis=2, tiled=True)  31.4 us
    ppermute x3, waiting for transfers between devices, shards(): lax.ppermute(sent, 'chan', [(i_2, (i_2 + lap) % size) for i_2 in range(si...  19.9 us
    all_gather x1, waiting for transfers between devices, shards(): shard_piece = lax.all_gather(beam_data, 'range', axis=3, tiled=True)  19.7 us
    all_to_all x1, blocking collectives, shards(): lax.all_to_all(compressed, 'pulse', split_axis=3, concat_axis=2, tiled=True)  17.2 us
    all_to_all x1, blocking collectives, shards(): lax.all_to_all(mixed_real * mixed_real + mixed_imag * mixed_imag, 'pulse'...  16.9 us
  transfers between devices with their start and end apart: 9, of which 8 were waited for; matrix products, arithmetic and copies ran while one was open for 4% of the time, Pallas kernels for 0%

profile of v1, /device:TPU:0, one launch (start us, length us, event | category | flops | bytes accessed | tf_op | source)
XLA Modules:
  0.0 389.7 jit_solution(9948941066630835210)
XLA Ops:
  6.5 4.1 %copy.35 = bf16[2,16,8,4096]{3,1,0,2:T(8,128)(2,1)} copy(bf16[2,16,8,4096]{3,2,1,0:T(8,128)(2,1)} %param.3) | data formatting | bytes 4194304 | tf_op args[0]
  10.6 6.5 %all-to-all-start = ((bf16[2,16,8,4096]{3,1,0,2:T(8,128)(2,1)}), bf16[2,16,8,4096]{3,1,0,2:T(8,128)(2,1)S(1)}, u32[]{:S(2)}, u32[]{:S(2)}) async-start(bf16[2,16,8,4096]{3,1,0,2:T(8,128)(2,1)} %copy.35), calls=%async_computation | async-start | bytes 4194304 | tf_op jit(solution)/shard_map/all_to_all | solution.py:118
  17.1 48.2 %all-to-all-done = bf16[2,16,8,4096]{3,1,0,2:T(8,128)(2,1)S(1)} async-done(((bf16[2,16,8,4096]{3,1,0,2:T(8,128)(2,1)}), bf16[2,16,8,4096]{3,1,0,2:T(8,128)(2,1)S(1)}, u32[]{:S(2)}, u32[]{:S(2)}) %all-to-all-start) | async-done | bytes 2097184 | tf_op jit(solution)/shard_map/all_to_all | solution.py:118
  65.3 2.2 copy.36
  69.5 3.7 collective-permute-start.2
  73.2 7.2 %collective-permute-done = bf16[1,2,8,2,4096]{4,2,3,0,1:T(8,128)(2,1)S(1)} collective-permute-done((bf16[1,2,8,2,4096]{4,2,3,0,1:T(8,128)(2,1)S(1)}, bf16[1,2,8,2,4096]{4,2,3,0,1:T(8,128)(2,1)S(1)}, u32[]{:S(2)}, u32[]{:S(2)}) %collective-permute-start) | collective-permute-done | bytes 262176 | tf_op jit(solution)/shard_map/ppermute | solution.py:130
  80.4 12.7 %collective-permute-done.1 = bf16[1,2,8,2,4096]{4,2,3,0,1:T(8,128)(2,1)S(1)} collective-permute-done((bf16[1,2,8,2,4096]{4,2,3,0,1:T(8,128)(2,1)S(1)}, bf16[1,2,8,2,4096]{4,2,3,0,1:T(8,128)(2,1)S(1)}, u32[]{:S(2)}, u32[]{:S(2)}) %collective-permute-start.1) | collective-permute-done | bytes 262176 | tf_op jit(solution)/shard_map/ppermute | solution.py:130
  95.1 6.4 %reshape.191 = f32[2,4096,2]{2,1,0:T(8,128)} reshape(f32[2,8192]{1,0:T(2,128)S(1)} %copy-done.1) | data formatting | bytes 131072 | tf_op jit(solution)/shard_map/reshape | solution.py:160
  101.5 4.8 %dynamic-slice_reduce_fusion = f32[2,4096]{1,0:T(2,128)S(1)} fusion(f32[2,4096,2]{2,1,0:T(8,128)} %reshape.191, s32[]{:T(128)S(6)} %select_n.191), kind=kLoop, calls=%fused_computation.31 | loop fusion | bytes 65540 | tf_op jit(solution)/shard_map/jit(dynamic_index_in_dim)/dynamic_slice | solution.py:161
  107.0 19.7 %all-gather.4.cloned.1.call-done = bf16[2,8,8,8192]{3,2,1,0:T(8,128)(2,1)} async-done(((bf16[2,8,8,4096]{3,2,1,0:T(8,128)(2,1)}), bf16[2,8,8,8192]{3,2,1,0:T(8,128)(2,1)}) %all-gather.4.cloned.1.call-update) | async-done | bytes 2097168 | tf_op jit(solution)/shard_map/all_gather | solution.py:140
  126.7 3.9 %fusion.275 = (f32[1,8,8,8192]{3,2,1,0:T(8,128)}, f32[1,8,8,8192]{3,2,1,0:T(8,128)}) fusion(bf16[2,8,8,8192]{3,2,1,0:T(8,128)(2,1)} %all-gather.4.cloned.1.call-done), kind=kLoop, calls=%fused_computation.370 | loop fusion | bytes 8388608 | tf_op jit(solution)/shard_map/slice | solution.py:151
  130.6 3.0 squeeze.26
  133.6 4.0 %squeeze.27 = f32[8,8,2,4096]{3,2,1,0:T(2,128)} reshape(f32[1,8,8,8192]{3,2,1,0:T(8,128)} %get-tuple-element.12) | data formatting | bytes 4194304 | tf_op jit(solution)/shard_map/squeeze | solution.py:151
  137.7 8.0 %subtract_reduce_fusion.1 = (f32[8,8,4096]{2,1,0:T(8,128)S(1)}, f32[8,8,4096]{2,1,0:T(8,128)S(1)}) fusion(f32[8,8,2,4096]{3,2,1,0:T(2,128)} %squeeze.27, f32[8,8,2,4096]{3,2,1,0:T(2,128)S(1)} %squeeze.26, f32[2]{0:T(128)S(1)} %get-tuple-element.23, f32[2]{0:T(128)S(1)} %get-tuple-element.22), kind=kLoop, calls=%fused_computation.35 | loop fusion | flops 3670016 | bytes 6291472 | tf_op jit(solution)/shard_map/reduce_sum | solution.py:151
  163.8 2.2 fusion
  166.0 2.4 reshape.194
  168.4 2.2 fusion.1
  172.1 1.6 multiply_subtract_fusion
  174.5 32.5 %all-gather.6.cloned.1.call-done = f32[8,8,8192]{2,1,0:T(8,128)} async-done(((f32[8,8,4096]{2,1,0:T(8,128)}), f32[8,8,8192]{2,1,0:T(8,128)}) %all-gather.6.cloned.1.call-update) | async-done | bytes 2097168 | tf_op jit(solution)/shard_map/all_gather | solution.py:169
  207.0 3.2 reshape.195
  210.2 31.4 %all-gather.8.cloned.1.call-done = f32[8,8,8192]{2,1,0:T(8,128)} async-done(((f32[8,8,4096]{2,1,0:T(8,128)}), f32[8,8,8192]{2,1,0:T(8,128)}) %all-gather.8.cloned.1.call-update) | async-done | bytes 2097168 | tf_op jit(solution)/shard_map/all_gather | solution.py:170
  241.6 4.0 %reshape.196 = f32[8,8,2,4096]{3,2,1,0:T(2,128)} reshape(f32[8,8,8192]{2,1,0:T(8,128)} %all-gather.8.cloned.1.call-done) | data formatting | bytes 4194304 | tf_op jit(solution)/shard_map/reshape | solution.py:174
  245.7 7.6 %subtract_reduce_fusion = (f32[8,8,4096]{2,1,0:T(8,128)S(1)}, f32[8,8,4096]{2,1,0:T(8,128)S(1)}) fusion(f32[8,8,2,4096]{3,2,1,0:T(2,128)} %reshape.196, f32[8,8,2,4096]{3,2,1,0:T(2,128)S(1)} %reshape.195, f32[2]{0:T(128)S(1)} %fusion.202, f32[2]{0:T(128)S(1)} %get-tuple-element.22), kind=kLoop, calls=%fused_computation.33 | loop fusion | flops 3670016 | bytes 6291472 | tf_op jit(solution)/shard_map/reduce_sum | solution.py:181
  253.5 13.8 %copy.42 = bf16[2,8,8,4096]{2,1,0,3:T(8,128)(2,1)} copy(bf16[2,8,8,4096]{3,2,1,0:T(8,128)(2,1)S(1)} %pad_maximum_fusion.2) | data formatting | bytes 2097152 | tf_op jit(solution)/shard_map/stack | solution.py:183
  267.3 20.5 %reshape.206 = bf16[4,2,65536]{2,1,0:T(2,128)(2,1)S(1)} reshape(bf16[4096,2,8,8]{3,2,1,0:T(8,128)(2,1)} %bitcast.153) | data formatting | bytes 2097152
  287.9 17.2 %all_to_all.48 = bf16[4,2,65536]{2,1,0:T(2,128)(2,1)S(1)} all-to-all(bf16[4,2,65536]{2,1,0:T(2,128)(2,1)S(1)} %reshape.206), channel_id=1, replica_groups=mesh['chan'=4,'pulse'=4,'range'=2] {'pulse'}, dimensions={0} | all-to-all | bytes 2097152 | tf_op jit(solution)/shard_map/all_to_all | solution.py:188
  305.1 21.7 %reshape.207 = bf16[4096,2,8,8]{3,2,1,0:T(8,128)(2,1)} reshape(bf16[4,2,65536]{2,1,0:T(2,128)(2,1)S(1)} %all_to_all.48) | data formatting | bytes 2097152
  326.8 16.0 %copy.43 = bf16[2,8,8,4,1024]{4,2,3,1,0:T(8,128)(2,1)S(1)} copy(bf16[2,8,8,4,1024]{2,1,0,4,3:T(8,128)(2,1)} %bitcast.154) | data formatting | bytes 2097152 | tf_op jit(solution)/shard_map/all_to_all | solution.py:188
  344.9 16.9 %all_to_all.49 = f32[8,32,1024]{2,0,1:T(8,128)S(1)} all-to-all(f32[8,32,1024]{2,0,1:T(8,128)S(1)} %copy.44), channel_id=1, replica_groups=mesh['chan'=4,'pulse'=4,'range'=2] {'pulse'}, dimensions={1} | all-to-all | bytes 2097152 | tf_op jit(solution)/shard_map/all_to_all | solution.py:195
  362.4 2.4 collective-permute-start.3
  366.4 4.2 %collective-permute-done.4 = f32[8,8,20]{2,1,0:T(8,128)S(1)} collective-permute-done((f32[8,8,20]{2,1,0:T(8,128)S(1)}, f32[8,8,20]{2,1,0:T(8,128)S(1)}, u32[]{:S(2)}, u32[]{:S(2)}) %collective-permute-start.4) | collective-permute-done | bytes 5152 | tf_op jit(solution)/shard_map/ppermute | solution.py:32
  370.7 12.0 %fusion.14 = f32[8,8,4096]{2,1,0:T(8,128)} fusion(f32[8,8,4096]{2,1,0:T(8,128)S(1)} %bitcast.174, f32[8,8,20]{2,1,0:T(8,128)S(1)} %collective-permute-done.4, f32[8,8,20]{2,1,0:T(8,128)S(1)} %collective-permute-done.3), kind=kLoop, calls=%fused_computation.60 | loop fusion | flops 17301504 | bytes 2107392 | tf_op jit(solution)/shard_map/div | solution.py:214
  (61 shorter events, 29.4 us)
Async XLA Ops:
  10.6 6.5 %copy-start.2 = (bf16[2,32,64]{2,1,0:T(8,128)(2,1)S(1)}, bf16[2,32,64]{2,1,0:T(8,128)(2,1)}, u32[]{:S(2)}) copy-start(bf16[2,32,64]{2,1,0:T(8,128)(2,1)} %param.4) | copy-start | bytes 24580
  10.6 54.7 %all-to-all-start = ((bf16[2,16,8,4096]{3,1,0,2:T(8,128)(2,1)}), bf16[2,16,8,4096]{3,1,0,2:T(8,128)(2,1)S(1)}, u32[]{:S(2)}, u32[]{:S(2)}) async-start(bf16[2,16,8,4096]{3,1,0,2:T(8,128)(2,1)} %copy.35), calls=%async_computation | async-start | bytes 4194304 | tf_op jit(solution)/shard_map/all_to_all | solution.py:118
  17.1 109.6 %all-gather.4.cloned.1.call-start = ((), (), s32[]{:S(2)}) async-start(), calls=%async_computation.3 | async-start | bytes 3145728 | tf_op jit(solution)/shard_map/all_gather | solution.py:140
  69.3 11.0 %collective-permute-start = (bf16[1,2,8,2,4096]{4,2,3,0,1:T(8,128)(2,1)S(1)}, bf16[1,2,8,2,4096]{4,2,3,0,1:T(8,128)(2,1)S(1)}, u32[]{:S(2)}, u32[]{:S(2)}) collective-permute-start(bf16[1,2,8,2,4096]{4,2,3,0,1:T(8,128)(2,1)S(1)} %get-tuple-element.17), channel_id=1, source_target_pairs={{0,8},{8,16},{16,24},{24,0},{1,9},{9,17},{17,25},{25,1},{2,10},{10... | collective-permute-start | bytes 786440 | tf_op jit(solution)/shard_map/ppermute | solution.py:130
  69.5 23.7 %collective-permute-start.2 = (bf16[1,2,8,2,4096]{4,2,3,0,1:T(8,128)(2,1)S(1)}, bf16[1,2,8,2,4096]{4,2,3,0,1:T(8,128)(2,1)S(1)}, u32[]{:S(2)}, u32[]{:S(2)}) collective-permute-start(bf16[1,2,8,2,4096]{4,2,3,0,1:T(8,128)(2,1)S(1)} %get-tuple-element.15), channel_id=1, source_target_pairs={{0,24},{8,0},{16,8},{24,16},{1,25},{9,1},{17,9},{25,17},{2,26},{10... | collective-permute-start | bytes 786440 | tf_op jit(solution)/shard_map/ppermute | solution.py:130
  73.2 19.9 %collective-permute-start.1 = (bf16[1,2,8,2,4096]{4,2,3,0,1:T(8,128)(2,1)S(1)}, bf16[1,2,8,2,4096]{4,2,3,0,1:T(8,128)(2,1)S(1)}, u32[]{:S(2)}, u32[]{:S(2)}) collective-permute-start(bf16[1,2,8,2,4096]{4,2,3,0,1:T(8,128)(2,1)S(1)} %get-tuple-element.16), channel_id=1, source_target_pairs={{0,16},{8,24},{16,0},{24,8},{1,17},{9,25},{17,1},{25,9},{2,18},{10... | collective-permute-start | bytes 786440 | tf_op jit(solution)/shard_map/ppermute | solution.py:130
  80.4 14.7 %copy-start.1 = (f32[2,8192]{1,0:T(2,128)S(1)}, f32[2,8192]{1,0:T(2,128)}, u32[]{:S(2)}) copy-start(f32[2,8192]{1,0:T(2,128)} %param.5) | copy-start | bytes 196612
  94.8 112.2 %all-gather.6.cloned.1.call-start = ((), (), s32[]{:S(2)}) async-start(), calls=%async_computation.4 | async-start | bytes 3145728 | tf_op jit(solution)/shard_map/all_gather | solution.py:169
  170.5 1.5 copy-start
  173.7 67.9 %all-gather.8.cloned.1.call-start = ((), (), s32[]{:S(2)}) async-start(), calls=%async_computation.5 | async-start | bytes 3145728 | tf_op jit(solution)/shard_map/all_gather | solution.py:170
  362.4 4.0 %collective-permute-start.3 = (f32[8,8,20]{2,1,0:T(8,128)S(1)}, f32[8,8,20]{2,1,0:T(8,128)S(1)}, u32[]{:S(2)}, u32[]{:S(2)}) collective-permute-start(f32[8,8,20]{2,1,0:T(8,128)S(1)} %get-tuple-element.13), channel_id=1, source_target_pairs={{0,1},{2,3},{4,5},{6,7},{8,9},{10,11},{12,13},{14,15},{16,17},{18,... | collective-permute-start | bytes 15368 | tf_op jit(solution)/shard_map/ppermute | solution.py:31
  364.9 5.8 %collective-permute-start.4 = (f32[8,8,20]{2,1,0:T(8,128)S(1)}, f32[8,8,20]{2,1,0:T(8,128)S(1)}, u32[]{:S(2)}, u32[]{:S(2)}) collective-permute-start(f32[8,8,20]{2,1,0:T(8,128)S(1)} %get-tuple-element.14), channel_id=1, source_target_pairs={{1,0},{3,2},{5,4},{7,6},{9,8},{11,10},{13,12},{15,14},{17,16},{19,... | collective-permute-start | bytes 15368 | tf_op jit(solution)/shard_map/ppermute | solution.py:32
Sparse Core Ops, SparseCore 0:
  94.9 31.6 all-gather.3
  173.8 33.0 all-gather.5
  208.5 33.0 all-gather.7
